TPU v7x, 32 devices: a whole 2x2x4 slice. The times are simulated.
32 devices in a mesh: batch: 4 (over x, core), lat: 8 (over z, y).
Axes of the slice: x: 2, y: 2, z: 4, core: 2. Of those that a mesh axis runs over, the one named last changes fastest.
Arguments:
- predicted: bfloat16 [4, 73, 192, 1440], P('batch', None, 'lat'), may hold values from -64 to 64
- target: bfloat16 [4, 73, 192, 1440], P('batch', None, 'lat'), may hold values from -128 to 128
- legendre_basis: bfloat16 [192, 96, 720], P(None, ('batch', 'lat')), may hold values from -1 to 1
Outputs:
- spectra: float32 [2, 73, 720], replicated
- channel_loss: float32 [73], replicated
All inputs are finite; a program needn't handle non-finite values.
Results may differ from a plain program's by a relative error of at most 0.0003.
Values may be sent and summed in bfloat16 or wider, within the bound.
No kernel may reach another device: no remote copies, remote signals or barrier semaphores. Data moves between devices by JAX's collectives and lax.ppermute only.
A program may use at most 128 MiB of HBM per device.

v0:
```python
import math
import jax
import jax.numpy as jnp
from jax import lax
from jax.sharding import PartitionSpec as P


def fourier_table(lon_count, order_count):
    lon_ids = jnp.arange(lon_count, dtype=jnp.int32)
    order_ids = jnp.arange(order_count, dtype=jnp.int32)
    product_ids = lon_ids[:, None] * order_ids[None, :] % lon_count
    angles = 2.0 * math.pi / lon_count * product_ids.astype(jnp.float32)
    inv_root = 1.0 / math.sqrt(lon_count)
    return jnp.stack([jnp.cos(angles) * inv_root, -jnp.sin(angles) * inv_root], axis=1).astype(
        jnp.bfloat16
    )


def band_energy(fourier, basis_block, orders):
    coefficients = jnp.einsum(
        "fpmbcn,nml->fpmbcl", fourier, basis_block, preferred_element_type=jnp.float32
    )
    squares = jnp.sum(coefficients * coefficients, axis=1)
    weights = jnp.where(orders == 0, 1.0, 2.0).astype(jnp.float32)
    return jnp.sum(squares * weights[None, :, None, None, None], axis=(1, 2))


def body(predicted, target, legendre_basis):
    groups = lax.axis_size("batch")
    band_count = lax.axis_size("lat")
    per_dev = legendre_basis.shape[1]
    order_count = per_dev * groups * band_count
    dft_table = fourier_table(predicted.shape[3], order_count)
    band_id = lax.axis_index("lat")

    def transform(field_in):
        return jnp.einsum(
            "bcnk,kpm->pmbcn", field_in, dft_table, preferred_element_type=jnp.float32
        ).astype(jnp.bfloat16)

    fourier = jnp.stack([transform(predicted), transform(target)], axis=0)
    members = fourier.shape[3]
    channels = fourier.shape[4]
    lat_rows = fourier.shape[5]
    fourier = fourier.reshape(2, 2, groups, band_count, per_dev, members, channels, lat_rows)
    arrived = lax.all_to_all(fourier, "lat", split_axis=3, concat_axis=7, tiled=True)
    arrived = arrived.reshape(
        2, 2, groups * per_dev, arrived.shape[5], arrived.shape[6], arrived.shape[7]
    )
    basis_block = lax.all_gather(legendre_basis, "batch", axis=1, tiled=True)
    taken = basis_block.shape[1]
    gathered_ids = jnp.arange(taken, dtype=jnp.int32)
    orders = (
        gathered_ids // per_dev * band_count * per_dev + band_id * per_dev + gathered_ids % per_dev
    )
    partial_value = band_energy(arrived, basis_block, orders)
    energy = lax.psum(partial_value, "lat")
    energy = lax.psum(energy, "batch")
    spectra = energy / (predicted.shape[0] * groups * order_count)
    log_spectra = jnp.log(spectra + 1e-06)
    channel_loss = jnp.mean((log_spectra[0] - log_spectra[1]) ** 2, axis=1)
    return (spectra, channel_loss)


def solution(mesh):
    placed = (
        P("batch", None, "lat", None),
        P("batch", None, "lat", None),
        P(None, ("batch", "lat"), None),
    )
    return jax.shard_map(body, mesh=mesh, in_specs=placed, out_specs=(P(), P()), check_vma=False)
```

profile of v0, /device:TPU:0, one launch (start us, length us, event | category | flops | bytes accessed | tf_op | source)
XLA Modules:
  0.0 212.2 jit_solution(11625327290755649896)
XLA Ops:
  7.2 0.0 all-gather.2.cloned.1.call-start
  7.2 0.7 all-gather.2.cloned.1.call-update
  7.9 2.6 %multiply_convert_fusion = (bf16[1440,1,96]{0,2,1:T(8,128)(2,1)S(1)}, bf16[1440,1,96]{0,2,1:T(8,128)(2,1)S(1)}) fusion(), kind=kLoop, calls=%fused_computation.17 | loop fusion | flops 1935360 | bytes 552960 | tf_op jit(solution)/shard_map/convert.1
  10.5 0.0 copy-start
  10.5 0.0 copy-start.1
  10.5 0.7 copy-done
  11.2 0.1 copy-done.1
  11.3 4.8 %fusion.8 = bf16[2,96,73,24]{1,2,3,0:T(8,128)(2,1)S(1)} fusion(bf16[73,24,1440]{2,1,0:T(8,128)(2,1)} %bitcast.33, bf16[1440,1,96]{0,2,1:T(8,128)(2,1)S(1)} %get-tuple-element.4, bf16[1440,1,96]{0,2,1:T(8,128)(2,1)S(1)} %get-tuple-element.5), kind=kOutput, calls=%fused_computation.11 | convolution fusion | flops 970228224 | bytes 6271488 | tf_op jit(solution)/shard_map/bcnk,kpm->pmbcn/dot_general | solution.py:37
  16.1 0.9 copy.29
  17.0 5.5 %fusion.11 = bf16[2,96,73,24]{1,2,3,0:T(8,128)(2,1)S(1)} fusion(bf16[73,24,1440]{2,1,0:T(8,128)(2,1)} %bitcast.34, bf16[1440,1,96]{0,2,1:T(8,128)(2,1)} %copy-done, bf16[1440,1,96]{0,2,1:T(8,128)(2,1)} %copy-done.1), kind=kOutput, calls=%fused_computation.12 | convolution fusion | flops 970228224 | bytes 6271488 | tf_op jit(solution)/shard_map/bcnk,kpm->pmbcn/dot_general | solution.py:37
  22.5 0.9 copy.31
  23.3 0.5 pad_maximum_fusion
  23.9 2.0 copy.32
  25.9 7.5 %all-to-all-start = ((bf16[2,2,4,8,3,1,73,24]{6,7,4,2,1,5,0,3:T(8,128)(2,1)}), bf16[2,2,4,8,3,1,73,24]{6,7,4,2,1,5,0,3:T(8,128)(2,1)S(1)}, u32[]{:S(2)}, u32[]{:S(2)}) async-start(bf16[2,2,4,8,3,1,73,24]{6,7,4,2,1,5,0,3:T(8,128)(2,1)} %copy.32), calls=%async_computation | async-start | bytes 4718592 | tf_op jit(solution)/shard_map/all_to_all | solution.py:46
  33.5 0.0 all-reduce.3.cloned.1.call-start
  33.5 53.6 %all-to-all-done = bf16[2,2,4,8,3,1,73,24]{6,7,4,2,1,5,0,3:T(8,128)(2,1)S(1)} async-done(((bf16[2,2,4,8,3,1,73,24]{6,7,4,2,1,5,0,3:T(8,128)(2,1)}), bf16[2,2,4,8,3,1,73,24]{6,7,4,2,1,5,0,3:T(8,128)(2,1)S(1)}, u32[]{:S(2)}, u32[]{:S(2)}) %all-to-all-start) | async-done | bytes 1345568 | tf_op jit(solution)/shard_map/all_to_all | solution.py:46
  87.1 2.1 copy.33
  89.2 0.0 all-gather.2.cloned.1.call-done
  89.2 5.1 %multiply_reduce_fusion = f32[12,2,73,720]{3,2,1,0:T(8,128)S(1)} fusion(bf16[192,12,720]{2,0,1:T(8,128)(2,1)} %all-gather.2.cloned.1.call-done, bf16[2,2,12,73,192]{3,4,2,1,0:T(8,128)(2,1)} %bitcast.30), kind=kOutput, calls=%fused_computation | convolution fusion | flops 972570240 | bytes 9709056 | tf_op jit(solution)/shard_map/fpmbcn,nml->fpmbcl/dot_general | solution.py:20
  94.3 0.6 multiply_reduce_fusion.1
  94.9 1.1 copy.40
  96.0 0.0 all-reduce.3.cloned.1.call-update
  96.1 0.0 all-reduce.5.cloned.1.call-start
  96.1 71.4 %all-reduce.3.cloned.1.call-done = f32[2,73,720]{2,0,1:T(2,128)} async-done(((f32[2,73,720]{2,0,1:T(2,128)}), f32[2,73,720]{2,0,1:T(2,128)}) %all-reduce.3.cloned.1.call-update) | async-done | bytes 420496 | tf_op jit(solution)/shard_map/psum | solution.py:57
  167.5 0.0 all-reduce.5.cloned.1.call-update
  167.6 34.7 %all-reduce.5.cloned.1.call-done = f32[2,73,720]{2,0,1:T(2,128)} async-done(((f32[2,73,720]{2,0,1:T(2,128)}), f32[2,73,720]{2,0,1:T(2,128)}) %all-reduce.5.cloned.1.call-update) | async-done | bytes 420496 | tf_op jit(solution)/shard_map/psum | solution.py:58
  202.2 2.2 %add_log_fusion = (f32[2,73,720]{2,0,1:T(2,128)S(1)}, f32[2,73,720]{2,0,1:T(2,128)}) fusion(f32[2,73,720]{2,0,1:T(2,128)} %all-reduce.5.cloned.1.call-done), kind=kLoop, calls=%fused_computation.23 | loop fusion | flops 210240 | bytes 1261440 | tf_op jit(solution)/shard_map/log | solution.py:60
  204.5 0.6 fusion.20
  205.1 0.5 broadcast_multiply_fusion.1
  (1 shorter events, 0.0 us)
Async XLA Ops:
  7.2 82.1 %all-gather.2.cloned.1.call-start = ((), (), s32[]{:S(2)}) async-start(), calls=%async_computation.1 | async-start | bytes 4423680 | tf_op jit(solution)/shard_map/all_gather | solution.py:50
  10.5 0.7 copy-start
  10.5 0.8 copy-start.1
  25.9 61.2 %all-to-all-start = ((bf16[2,2,4,8,3,1,73,24]{6,7,4,2,1,5,0,3:T(8,128)(2,1)}), bf16[2,2,4,8,3,1,73,24]{6,7,4,2,1,5,0,3:T(8,128)(2,1)S(1)}, u32[]{:S(2)}, u32[]{:S(2)}) async-start(bf16[2,2,4,8,3,1,73,24]{6,7,4,2,1,5,0,3:T(8,128)(2,1)} %copy.32), calls=%async_computation | async-start | bytes 4718592 | tf_op jit(solution)/shard_map/all_to_all | solution.py:46
  33.5 134.1 %all-reduce.3.cloned.1.call-start = ((), (), s32[]{:S(2)}) async-start(), calls=%async_computation.2 | async-start | bytes 897024 | tf_op jit(solution)/shard_map/psum | solution.py:57
  96.1 106.2 %all-reduce.5.cloned.1.call-start = ((), (), s32[]{:S(2)}) async-start(), calls=%async_computation.3 | async-start | bytes 897024 | tf_op jit(solution)/shard_map/psum | solution.py:58
Sparse Core Ops, SparseCore 0:
  9.5 33.4 all-gather.1
  96.2 71.2 all-reduce.2
  169.9 32.2 all-reduce.4
where the time goes:
time: 212 us
  waiting for transfers between devices  160 us (75%)
  matrix products  15.4 us (7%)
  between operations  13.8 us (7%)
  local copies, waits for them, and re-layouts  7.77 us (4%)
  starting transfers between devices  7.66 us (4%)
  other arithmetic  7.07 us (3%)
    psum x1, waiting for transfers between devices, body(): energy = lax.psum(partial_value, 'lat')  71.4 us
    all_to_all x1, waiting for transfers between devices, body(): lax.all_to_all(fourier, 'lat', split_axis=3, concat_axis=7, tiled=True)  53.6 us
    psum x1, waiting for transfers between devices, body(): energy = lax.psum(energy, 'batch')  34.7 us
    dot_general x2, matrix products, transform(): jnp.einsum('bcnk,kpm->pmbcn', field_in, dft_table, preferred_element_type...  10.3 us
    all_to_all x1, starting transfers between devices, body(): lax.all_to_all(fourier, 'lat', split_axis=3, concat_axis=7, tiled=True)  7.55 us
    dot_general x1, matrix products, band_energy(): jnp.einsum('fpmbcn,nml->fpmbcl', fourier, basis_block, preferred_element_...  5.1 us
  transfers between devices with their start and end apart: 4, of which 3 were waited for; matrix products, arithmetic and copies ran while one was open for 9% of the time, Pallas kernels for 0%

commit v1 on v0

--- a/solution.py
+++ b/solution.py
@@ -43,7 +43,12 @@
     channels = fourier.shape[4]
     lat_rows = fourier.shape[5]
     fourier = fourier.reshape(2, 2, groups, band_count, per_dev, members, channels, lat_rows)
-    arrived = lax.all_to_all(fourier, "lat", split_axis=3, concat_axis=7, tiled=True)
+    arrived = jnp.concatenate(
+        jax.lax.all_to_all(
+            jnp.stack(jnp.split(fourier, jax.lax.axis_size("lat"), 3), axis=0), "lat", 0, 0
+        ),
+        7,
+    )
     arrived = arrived.reshape(
         2, 2, groups * per_dev, arrived.shape[5], arrived.shape[6], arrived.shape[7]
     )

time: 212 us -> 216 us (1.019)
  other arithmetic: 7.07 us -> 12.8 us
    unnamed x0 -> x7, other arithmetic: none -> 5.44 us
  transfers between devices with their start and end apart: 4 -> 4, of which waited for: 3 -> 3; matrix products, arithmetic and copies ran while one was open for 9% -> 11% of each run, Pallas kernels for 0% -> 0%
where the time goes in v1:
time: 216 us
  waiting for transfers between devices  160 us (74%)
  matrix products  15.4 us (7%)
  between operations  13.8 us (6%)
  other arithmetic  12.8 us (6%)
  starting transfers between devices  7.66 us (4%)
  local copies, waits for them, and re-layouts  5.73 us (3%)
    psum x1, waiting for transfers between devices, body(): energy = lax.psum(partial_value, 'lat')  71.4 us
    all_to_all x1, waiting for transfers between devices, body(): jax.lax.all_to_all(jnp.stack(jnp.split(fourier, jax.lax.axis_size('lat'),...  53.6 us
    psum x1, waiting for transfers between devices, body(): energy = lax.psum(energy, 'batch')  34.7 us
    dot_general x2, matrix products, transform(): jnp.einsum('bcnk,kpm->pmbcn', field_in, dft_table, preferred_element_type...  10.3 us
    all_to_all x1, starting transfers between devices, body(): jax.lax.all_to_all(jnp.stack(jnp.split(fourier, jax.lax.axis_size('lat'),...  7.55 us
    unnamed x7, other arithmetic  5.44 us
    dot_general x1, matrix products, band_energy(): jnp.einsum('fpmbcn,nml->fpmbcl', fourier, basis_block, preferred_element_...  5.1 us
  transfers between devices with their start and end apart: 4, of which 3 were waited for; matrix products, arithmetic and copies ran while one was open for 11% of the time, Pallas kernels for 0%

profile of v1, /device:TPU:0, one launch (start us, length us, event | category | flops | bytes accessed | tf_op | source)
XLA Modules:
  0.0 215.8 jit_solution(8403773858691226363)
XLA Ops:
  7.2 0.0 all-gather.2.cloned.1.call-start
  7.2 0.7 all-gather.2.cloned.1.call-update
  7.9 2.6 %multiply_convert_fusion = (bf16[1440,1,96]{0,2,1:T(8,128)(2,1)S(1)}, bf16[1440,1,96]{0,2,1:T(8,128)(2,1)S(1)}) fusion(), kind=kLoop, calls=%fused_computation.30 | loop fusion | flops 1935360 | bytes 552960 | tf_op jit(solution)/shard_map/convert.1
  10.5 0.0 copy-start
  10.5 0.0 copy-start.1
  10.5 0.7 copy-done
  11.2 0.1 copy-done.1
  11.3 4.8 %fusion.8 = bf16[2,96,73,24]{1,2,3,0:T(8,128)(2,1)S(1)} fusion(bf16[73,24,1440]{2,1,0:T(8,128)(2,1)} %bitcast.77, bf16[1440,1,96]{0,2,1:T(8,128)(2,1)S(1)} %get-tuple-element.4, bf16[1440,1,96]{0,2,1:T(8,128)(2,1)S(1)} %get-tuple-element.5), kind=kOutput, calls=%fused_computation.24 | convolution fusion | flops 970228224 | bytes 6271488 | tf_op jit(solution)/shard_map/bcnk,kpm->pmbcn/dot_general | solution.py:37
  16.1 0.9 copy.55
  17.0 5.5 %fusion.11 = bf16[2,96,73,24]{1,2,3,0:T(8,128)(2,1)S(1)} fusion(bf16[73,24,1440]{2,1,0:T(8,128)(2,1)} %bitcast.78, bf16[1440,1,96]{0,2,1:T(8,128)(2,1)} %copy-done, bf16[1440,1,96]{0,2,1:T(8,128)(2,1)} %copy-done.1), kind=kOutput, calls=%fused_computation.25 | convolution fusion | flops 970228224 | bytes 6271488 | tf_op jit(solution)/shard_map/bcnk,kpm->pmbcn/dot_general | solution.py:37
  22.5 0.9 copy.57
  23.3 0.8 bitcast_dynamic-update-slice_fusion.5
  24.1 0.8 bitcast_dynamic-update-slice_fusion.4
  24.9 0.8 bitcast_dynamic-update-slice_fusion.3
  25.7 0.8 bitcast_dynamic-update-slice_fusion.2
  26.5 0.8 bitcast_dynamic-update-slice_fusion.1
  27.2 0.8 bitcast_dynamic-update-slice_fusion
  28.0 0.8 bitcast_dynamic-update-slice_fusion.6
  28.8 0.8 fusion.27
  29.6 7.5 %all-to-all-start = ((bf16[8,2,2,4,1,3,1,73,24]{7,8,5,3,2,1,6,4,0:T(8,128)(2,1)}), bf16[8,2,2,4,1,3,1,73,24]{7,8,5,3,2,1,6,4,0:T(8,128)(2,1)S(1)}, u32[]{:S(2)}, u32[]{:S(2)}) async-start(bf16[8,2,2,4,1,3,1,73,24]{7,8,5,3,2,1,6,4,0:T(8,128)(2,1)} %fusion.27), calls=%async_computation | async-start | bytes 4718592 | tf_op jit(solution)/shard_map/all_to_all | solution.py:47
  37.1 0.0 all-reduce.3.cloned.1.call-start
  37.2 53.6 %all-to-all-done = bf16[8,2,2,4,1,3,1,73,24]{7,8,5,3,2,1,6,4,0:T(8,128)(2,1)S(1)} async-done(((bf16[8,2,2,4,1,3,1,73,24]{7,8,5,3,2,1,6,4,0:T(8,128)(2,1)}), bf16[8,2,2,4,1,3,1,73,24]{7,8,5,3,2,1,6,4,0:T(8,128)(2,1)S(1)}, u32[]{:S(2)}, u32[]{:S(2)}) %all-to-all-start) | async-done | bytes 1345568 | tf_op jit(solution)/shard_map/all_to_all | solution.py:47
  90.8 2.1 copy.65
  92.9 0.0 all-gather.2.cloned.1.call-done
  92.9 5.1 %multiply_reduce_fusion = f32[12,2,73,720]{3,2,1,0:T(8,128)S(1)} fusion(bf16[192,12,720]{2,0,1:T(8,128)(2,1)} %all-gather.2.cloned.1.call-done, bf16[2,2,12,73,192]{3,4,2,1,0:T(8,128)(2,1)} %bitcast.76), kind=kOutput, calls=%fused_computation | convolution fusion | flops 972570240 | bytes 9709056 | tf_op jit(solution)/shard_map/fpmbcn,nml->fpmbcl/dot_general | solution.py:20
  98.0 0.6 multiply_reduce_fusion.1
  98.6 1.1 copy.72
  99.7 0.0 all-reduce.3.cloned.1.call-update
  99.7 0.0 all-reduce.5.cloned.1.call-start
  99.8 71.4 %all-reduce.3.cloned.1.call-done = f32[2,73,720]{2,0,1:T(2,128)} async-done(((f32[2,73,720]{2,0,1:T(2,128)}), f32[2,73,720]{2,0,1:T(2,128)}) %all-reduce.3.cloned.1.call-update) | async-done | bytes 420496 | tf_op jit(solution)/shard_map/psum | solution.py:62
  171.2 0.0 all-reduce.5.cloned.1.call-update
  171.2 34.7 %all-reduce.5.cloned.1.call-done = f32[2,73,720]{2,0,1:T(2,128)} async-done(((f32[2,73,720]{2,0,1:T(2,128)}), f32[2,73,720]{2,0,1:T(2,128)}) %all-reduce.5.cloned.1.call-update) | async-done | bytes 420496 | tf_op jit(solution)/shard_map/psum | solution.py:63
  205.9 2.2 %add_log_fusion = (f32[2,73,720]{2,0,1:T(2,128)S(1)}, f32[2,73,720]{2,0,1:T(2,128)}) fusion(f32[2,73,720]{2,0,1:T(2,128)} %all-reduce.5.cloned.1.call-done), kind=kLoop, calls=%fused_computation.36 | loop fusion | flops 210240 | bytes 1261440 | tf_op jit(solution)/shard_map/log | solution.py:65
  208.1 0.6 fusion.29
  208.8 0.5 broadcast_multiply_fusion.1
  (1 shorter events, 0.0 us)
Async XLA Ops:
  7.2 85.7 %all-gather.2.cloned.1.call-start = ((), (), s32[]{:S(2)}) async-start(), calls=%async_computation.1 | async-start | bytes 4423680 | tf_op jit(solution)/shard_map/all_gather | solution.py:55
  10.5 0.7 copy-start
  10.5 0.8 copy-start.1
  29.6 61.2 %all-to-all-start = ((bf16[8,2,2,4,1,3,1,73,24]{7,8,5,3,2,1,6,4,0:T(8,128)(2,1)}), bf16[8,2,2,4,1,3,1,73,24]{7,8,5,3,2,1,6,4,0:T(8,128)(2,1)S(1)}, u32[]{:S(2)}, u32[]{:S(2)}) async-start(bf16[8,2,2,4,1,3,1,73,24]{7,8,5,3,2,1,6,4,0:T(8,128)(2,1)} %fusion.27), calls=%async_computation | async-start | bytes 4718592 | tf_op jit(solution)/shard_map/all_to_all | solution.py:47
  37.1 134.1 %all-reduce.3.cloned.1.call-start = ((), (), s32[]{:S(2)}) async-start(), calls=%async_computation.2 | async-start | bytes 897024 | tf_op jit(solution)/shard_map/psum | solution.py:62
  99.7 106.2 %all-reduce.5.cloned.1.call-start = ((), (), s32[]{:S(2)}) async-start(), calls=%async_computation.3 | async-start | bytes 897024 | tf_op jit(solution)/shard_map/psum | solution.py:63
Sparse Core Ops, SparseCore 0:
  9.5 33.4 all-gather.1
  99.8 71.2 all-reduce.2
  173.5 32.2 all-reduce.4
